TPU v7x, 512 devices: a 4x2x32 block of a 4x8x32 slice. The times are simulated.
512 devices in a mesh: groups: 2 (over y), src: 64 (over z, core), act: 4 (over x).
Axes of the slice: x: 4, y: 2, z: 32, core: 2. Of those that a mesh axis runs over, the one named last changes fastest.
The devices are a block of a 4x8x32 slice.
Arguments:
- star_state: float32 [12, 65536], P(None, ('groups', 'src')), parts along dimension 1, may hold values from -6 to 6
- masses: float32 [65536], P(('groups', 'src')), parts along dimension 0, may hold values from 0.25 to 4
- phases: float32 [65536], P(('groups', 'src')), parts along dimension 0, may hold values from 0 to 1
- levels: int32 [65536], P(('groups', 'src')), parts along dimension 0, may hold values from 0 to 4, as said below
- active_list: int32 [32768], P(('groups', 'src', 'act')), parts along dimension 0, may hold values from 0 to 511, as said below
- active_count: int32 [512], P(('groups', 'src', 'act')), parts along dimension 0, may hold values from 0 to 64, as said below
Outputs:
- stepped_state: float32 [12, 65536], P(None, ('groups', 'src')), parts along dimension 1
There are 2 independent parts, one for each index of `groups`. A program takes and returns all parts, laid end to end along the dimension named above; each array names one. Nothing has to cross between parts.
Inputs may be any that keep to these rules, and one draw needn't show every extreme that they name: `levels`: levels_j = 4 exactly for the stars that appear among the live entries of the lists. `active_list`: live entries (the first active_count ones of a device's 64) are distinct indices within the device's src shard; every active star of a shard is live in exactly one list of that shard's 4 devices; later slots hold arbitrary indices of the shard. `active_count`: at most 64 a device, reached in every draw; the counts of one src shard's devices sum to at most 128, reached by some shard in every draw.
All inputs are finite; a program needn't handle non-finite values.
Results may differ from a plain program's by a relative error of at most 0.0003.
Values sent between devices are 32-bit elements; how exact they have to be, the bound alone decides.
A program may use at most 64 MiB of HBM per device.

v0:
```python
import jax
import jax.numpy as jnp
from jax import lax
from jax.sharding import PartitionSpec as P

LEVELS = 5
STEPS = 2


soften_sq = 0.0004
fine_step = 0.03125


def in_order(parts, dim):
    parts = jnp.moveaxis(parts, 0, dim)
    lengths = parts.shape
    return parts.reshape(*lengths[:dim], lengths[dim] * lengths[dim + 1], *lengths[dim + 2 :])


def one_gather(arrays, axis, dims):
    vector = jnp.concatenate([a.reshape(-1) for a in arrays])
    lines, at, finished = (lax.all_gather(vector, axis), 0, [])
    for a, dim in zip(arrays, dims):
        parts = lines[:, at : at + a.size].reshape(-1, *a.shape)
        finished.append(in_order(parts, dim))
        at += a.size
    return tuple(finished)


def sent_to_all(value, axis):
    copies = jnp.broadcast_to(value, (lax.axis_size(axis), *value.shape))
    return lax.all_to_all(copies, axis, split_axis=0, concat_axis=0, tiled=True)


def gathered_copies(value, axis, dim):
    parts = sent_to_all(value, axis)
    return in_order(parts, dim)


def in_blocks(value, dim, length):
    lengths = value.shape
    parts = value.reshape(*lengths[:dim], length, lengths[dim] // length, *lengths[dim + 1 :])
    return jnp.moveaxis(parts, dim, 0)


def sum_at_owner(value, axis, dim):
    length = lax.axis_size(axis)
    parts = lax.all_to_all(in_blocks(value, dim, length), axis, 0, 0, tiled=True)
    return jnp.sum(parts, axis=0)


def predict(star_state, elapsed):
    interval = elapsed[None, :]
    position = star_state[0:3] + interval * (
        star_state[3:6] + interval * (0.5 * star_state[6:9] + interval * star_state[9:12] / 6.0)
    )
    velocity = star_state[3:6] + interval * (star_state[6:9] + 0.5 * interval * star_state[9:12])
    return jnp.concatenate([position, velocity], axis=0)


def pair_block(targets, sources):
    delta_pos = sources[0:3, None, :] - targets[0:3, :, None]
    delta_vel = sources[3:6, None, :] - targets[3:6, :, None]
    dist_sq = (
        delta_pos[0] * delta_pos[0]
        + delta_pos[1] * delta_pos[1]
        + delta_pos[2] * delta_pos[2]
        + soften_sq
    )
    inverse = lax.rsqrt(dist_sq)
    inv_sq = inverse * inverse
    weight = sources[6][None, :] * inverse * inv_sq
    radial = (
        (delta_pos[0] * delta_vel[0] + delta_pos[1] * delta_vel[1] + delta_pos[2] * delta_vel[2])
        * inv_sq
        * 3.0
    )
    acceleration = jnp.sum(weight[None] * delta_pos, axis=2)
    jerk_sum = jnp.sum(weight[None] * (delta_vel - radial[None] * delta_pos), axis=2)
    return jnp.concatenate([acceleration, jerk_sum], axis=0)


def over_sources(targets, sources):
    return pair_block(targets, sources)


def pair_forces(targets, sources):
    count_tgt = targets.shape[1]
    width = 512
    blocks = targets.reshape(6, count_tgt // width, width).transpose(1, 0, 2)
    result = lax.map(lambda portion: over_sources(portion, sources), blocks)
    return result.transpose(1, 0, 2).reshape(6, count_tgt)


def correct(old_state, predicted_rows, forces):
    acc_old = old_state[6:9]
    jerk_old = old_state[9:12]
    acc_new = forces[0:3]
    jerk_new = forces[3:6]
    snap_term = (-6.0 * (acc_old - acc_new) - fine_step * (4.0 * jerk_old + 2.0 * jerk_new)) / (
        fine_step * fine_step
    )
    crackle = (12.0 * (acc_old - acc_new) + 6.0 * fine_step * (jerk_old + jerk_new)) / (
        fine_step * fine_step * fine_step
    )
    position = (
        predicted_rows[0:3] + fine_step**4 / 24.0 * snap_term + fine_step**5 / 120.0 * crackle
    )
    velocity = predicted_rows[3:6] + fine_step**3 / 6.0 * snap_term + fine_step**4 / 24.0 * crackle
    return jnp.concatenate([position, velocity, acc_new, jerk_new], axis=0)


def per_device(star_state, masses, phases, levels, active_list, active_count):
    shard_size = star_state.shape[1]
    total_stars = shard_size * lax.axis_size("src")
    weights = masses / total_stars
    slot_count = active_list.shape[0]
    lists_all, counts_all = one_gather((active_list, active_count), "act", (0, 0))
    act_count = counts_all.shape[0]
    half_slots = slot_count // 2
    list_ends = jnp.cumsum(counts_all)
    list_starts = list_ends - counts_all
    total_live = list_ends[-1]
    wanted = lax.axis_index("act") * half_slots + jnp.arange(half_slots, dtype=jnp.int32)
    owners = jnp.sum((wanted[:, None] >= list_ends[None, :]).astype(jnp.int32), axis=1)
    owners = jnp.minimum(owners, act_count - 1)
    picked = owners[:, None] == jnp.arange(act_count, dtype=jnp.int32)[None, :]
    begins = jnp.sum(jnp.where(picked, list_starts[None, :], 0), axis=1)
    position = owners * slot_count + wanted - begins
    table_index = jnp.arange(act_count * slot_count, dtype=jnp.int32)
    members = jnp.sum(
        jnp.where(position[:, None] == table_index[None, :], lists_all[None, :], 0), axis=1
    )
    live = wanted < total_live
    write_index = jnp.where(live, members, shard_size)
    tick_count = jnp.left_shift(jnp.int32(1), LEVELS - 1 - levels).astype(jnp.float32)
    state_now = star_state
    for substep in range(STEPS):
        elapsed = (
            jnp.where(levels == LEVELS - 1, 1.0, phases * (tick_count - STEPS) + (substep + 1))
            * fine_step
        )
        predicted = predict(state_now, elapsed)
        sources = jnp.concatenate([predicted, weights[None, :]], axis=0)
        targets = predicted[:, members]
        partial_terms = pair_forces(gathered_copies(targets, "src", 1), sources)
        forces = sum_at_owner(partial_terms, "src", 1)
        new_state = correct(state_now[:, members], targets, forces)
        all_new, all_index = (
            gathered_copies(new_state, "act", 1),
            gathered_copies(write_index, "act", 0),
        )
        state_now = state_now.at[:, all_index].set(all_new, mode="drop")
    return state_now


def solution(mesh):
    in_specs = (
        P(None, ("groups", "src")),
        P(("groups", "src")),
        P(("groups", "src")),
        P(("groups", "src")),
        P(("groups", "src", "act")),
        P(("groups", "src", "act")),
    )
    out_specs = P(None, ("groups", "src"))
    return jax.shard_map(
        per_device, mesh=mesh, in_specs=in_specs, out_specs=out_specs, check_vma=False
    )
```

profile of v0, /device:TPU:33, one launch (start us, length us, event | category | flops | bytes accessed | tf_op | source)
XLA Modules:
  0.0 239.5 jit_solution(17835953257977336483)
XLA Ops:
  0.7 1.3 dynamic-slice
  2.6 0.8 add_dynamic-update-slice_fusion
  3.4 8.0 %all-reduce = s32[260]{0:T(512)S(1)} all-reduce(s32[260]{0:T(512)S(1)} %add_dynamic-update-slice_fusion), channel_id=2, replica_groups=mesh['groups'=2,'src'=64,'act'=4] {'act'}, use_global_device_ids=true, to_apply=%add | all-reduce | flops 260 | bytes 2080
  12.3 0.7 fusion.14
  13.0 0.8 multiply_add_fusion.2
  14.7 0.8 reshape.195
  15.5 48.6 %all-to-all-start.1 = ((f32[64,1,192]{2,1,0:T(1,128)}), f32[64,1,192]{2,1,0:T(1,128)S(1)}, u32[]{:S(2)}, u32[]{:S(2)}) async-start(f32[64,1,192]{2,1,0:T(1,128)} %reshape.195), calls=%async_computation.1 | async-start | bytes 131072 | tf_op jit(solution)/shard_map/all_to_all | solution.py:32
  65.3 0.7 broadcast_multiply_fusion
  66.0 23.6 %all-to-all-done.1 = f32[64,1,192]{2,1,0:T(1,128)S(1)} async-done(((f32[64,1,192]{2,1,0:T(1,128)}), f32[64,1,192]{2,1,0:T(1,128)S(1)}, u32[]{:S(2)}, u32[]{:S(2)}) %all-to-all-start.1) | async-done | bytes 49184 | tf_op jit(solution)/shard_map/all_to_all | solution.py:32
  90.2 3.3 %all-to-all-start = ((s32[4,1,32]{2,1,0:T(1,128)}), s32[4,1,32]{2,1,0:T(1,128)S(1)}, u32[]{:S(2)}, u32[]{:S(2)}) async-start(s32[4,1,32]{2,1,0:T(1,128)} %broadcast_in_dim.99), calls=%async_computation | async-start | bytes 4096 | tf_op jit(solution)/shard_map/all_to_all | solution.py:32
  94.0 0.8 reduce.7
  95.1 11.0 %while.20 = (s32[]{:T(128)}, f32[4,6,512]{2,1,0:T(8,128)S(1)}, f32[1,512]{1,0:T(1,128)S(1)}, f32[3,512]{1,0:T(4,128)S(1)}, f32[4,6,512]{2,0,1:T(4,128)S(1)}, /*i...) while((s32[]{:T(128)}, f32[4,6,512]{2,1,0:T(8,128)S(1)}, f32[1,512]{1,0:T(1,128)S(1)}, ...), condition=%wide.region_7.8_spmd, body=%wide.region_4.7_spmd.sunk | while | flops 12058627 | bytes 16922740 | solution.py:91
  95.7 0.8 fusion.23
  96.5 1.4 multiply_reduce_fusion.6
  98.4 0.8 fusion.23
  99.2 1.4 multiply_reduce_fusion.6
  101.2 0.8 fusion.23
  102.0 1.4 multiply_reduce_fusion.6
  103.9 0.8 fusion.23
  104.7 1.4 multiply_reduce_fusion.6
  106.4 0.8 reshape.197
  107.2 5.6 %all-to-all-start.2 = ((f32[64,1,192]{2,1,0:T(1,128)}), f32[64,1,192]{2,1,0:T(1,128)S(1)}, u32[]{:S(2)}, u32[]{:S(2)}) async-start(f32[64,1,192]{2,1,0:T(1,128)} %reshape.197), calls=%async_computation.2 | async-start | bytes 131072 | tf_op jit(solution)/shard_map/all_to_all | solution.py:48
  114.9 22.5 %all-to-all-done.2 = f32[64,1,192]{2,1,0:T(1,128)S(1)} async-done(((f32[64,1,192]{2,1,0:T(1,128)}), f32[64,1,192]{2,1,0:T(1,128)S(1)}, u32[]{:S(2)}, u32[]{:S(2)}) %all-to-all-start.2) | async-done | bytes 49184 | tf_op jit(solution)/shard_map/all_to_all | solution.py:48
  137.3 0.8 reduce.8
  138.3 0.7 reshape.199
  139.0 4.4 %all-to-all-start.3 = ((f32[4,1,384]{2,1,0:T(1,128)}), f32[4,1,384]{2,1,0:T(1,128)S(1)}, u32[]{:S(2)}, u32[]{:S(2)}) async-start(f32[4,1,384]{2,1,0:T(1,128)} %reshape.199), calls=%async_computation.3 | async-start | bytes 12288 | tf_op jit(solution)/shard_map/all_to_all | solution.py:32
  143.5 4.2 %all-to-all-done.3 = f32[4,1,384]{2,1,0:T(1,128)S(1)} async-done(((f32[4,1,384]{2,1,0:T(1,128)}), f32[4,1,384]{2,1,0:T(1,128)S(1)}, u32[]{:S(2)}, u32[]{:S(2)}) %all-to-all-start.3) | async-done | bytes 6176 | tf_op jit(solution)/shard_map/all_to_all | solution.py:32
  148.5 1.0 scatter_fusion
  151.2 0.8 reshape.201
  152.0 8.2 %all-to-all-start.4 = ((f32[64,1,192]{2,1,0:T(1,128)}), f32[64,1,192]{2,1,0:T(1,128)S(1)}, u32[]{:S(2)}, u32[]{:S(2)}) async-start(f32[64,1,192]{2,1,0:T(1,128)} %reshape.201), calls=%async_computation.4 | async-start | bytes 131072 | tf_op jit(solution)/shard_map/all_to_all | solution.py:32
  160.2 24.7 %all-to-all-done.4 = f32[64,1,192]{2,1,0:T(1,128)S(1)} async-done(((f32[64,1,192]{2,1,0:T(1,128)}), f32[64,1,192]{2,1,0:T(1,128)S(1)}, u32[]{:S(2)}, u32[]{:S(2)}) %all-to-all-start.4) | async-done | bytes 49184 | tf_op jit(solution)/shard_map/all_to_all | solution.py:32
  184.9 0.8 reduce.10
  185.9 11.0 %while.21 = (s32[]{:T(128)}, f32[4,6,512]{2,1,0:T(8,128)S(1)}, f32[1,512]{1,0:T(1,128)S(1)}, f32[3,512]{1,0:T(4,128)S(1)}, f32[4,6,512]{2,0,1:T(4,128)S(1)}, /*i...) while((s32[]{:T(128)}, f32[4,6,512]{2,1,0:T(8,128)S(1)}, f32[1,512]{1,0:T(1,128)S(1)}, ...), condition=%wide.region_13.14_spmd, body=%wide.region_10.13_spmd.sunk | while | flops 12058627 | bytes 16922740 | solution.py:91
  186.5 0.8 fusion.25
  187.3 1.4 multiply_reduce_fusion.7
  189.2 0.8 fusion.25
  190.0 1.4 multiply_reduce_fusion.7
  192.0 0.8 fusion.25
  192.8 1.4 multiply_reduce_fusion.7
  194.8 0.8 fusion.25
  195.6 1.4 multiply_reduce_fusion.7
  197.3 0.8 reshape.203
  198.0 6.6 %all-to-all-start.5 = ((f32[64,1,192]{2,1,0:T(1,128)}), f32[64,1,192]{2,1,0:T(1,128)S(1)}, u32[]{:S(2)}, u32[]{:S(2)}) async-start(f32[64,1,192]{2,1,0:T(1,128)} %reshape.203), calls=%async_computation.5 | async-start | bytes 131072 | tf_op jit(solution)/shard_map/all_to_all | solution.py:48
  205.3 23.9 %all-to-all-done.5 = f32[64,1,192]{2,1,0:T(1,128)S(1)} async-done(((f32[64,1,192]{2,1,0:T(1,128)}), f32[64,1,192]{2,1,0:T(1,128)S(1)}, u32[]{:S(2)}, u32[]{:S(2)}) %all-to-all-start.5) | async-done | bytes 49184 | tf_op jit(solution)/shard_map/all_to_all | solution.py:48
  229.2 0.8 reduce.11
  230.3 6.5 %all_to_all.37 = f32[4,1,384]{2,1,0:T(1,128)S(1)} all-to-all(f32[4,1,384]{2,1,0:T(1,128)S(1)} %reshape.205), channel_id=1, replica_groups=mesh['groups'=2,'src'=64,'act'=4] {'act'}, dimensions={0} | all-to-all | bytes 12288 | tf_op jit(solution)/shard_map/all_to_all | solution.py:32
  237.7 1.0 scatter_fusion.1
  238.8 0.7 copy.235
  (125 shorter events, 15.9 us)
Async XLA Ops:
  15.5 74.1 %all-to-all-start.1 = ((f32[64,1,192]{2,1,0:T(1,128)}), f32[64,1,192]{2,1,0:T(1,128)S(1)}, u32[]{:S(2)}, u32[]{:S(2)}) async-start(f32[64,1,192]{2,1,0:T(1,128)} %reshape.195), calls=%async_computation.1 | async-start | bytes 131072 | tf_op jit(solution)/shard_map/all_to_all | solution.py:32
  90.2 17.1 %all-to-all-start = ((s32[4,1,32]{2,1,0:T(1,128)}), s32[4,1,32]{2,1,0:T(1,128)S(1)}, u32[]{:S(2)}, u32[]{:S(2)}) async-start(s32[4,1,32]{2,1,0:T(1,128)} %broadcast_in_dim.99), calls=%async_computation | async-start | bytes 4096 | tf_op jit(solution)/shard_map/all_to_all | solution.py:32
  95.1 17.7 %copy-start = (f32[12,512]{1,0:T(8,128)S(1)}, f32[12,512]{1,0:T(8,128)}, u32[]{:S(2)}) copy-start(f32[12,512]{1,0:T(8,128)} %param.10) | copy-start | bytes 73732
  107.2 30.1 %all-to-all-start.2 = ((f32[64,1,192]{2,1,0:T(1,128)}), f32[64,1,192]{2,1,0:T(1,128)S(1)}, u32[]{:S(2)}, u32[]{:S(2)}) async-start(f32[64,1,192]{2,1,0:T(1,128)} %reshape.197), calls=%async_computation.2 | async-start | bytes 131072 | tf_op jit(solution)/shard_map/all_to_all | solution.py:48
  139.0 8.6 %all-to-all-start.3 = ((f32[4,1,384]{2,1,0:T(1,128)}), f32[4,1,384]{2,1,0:T(1,128)S(1)}, u32[]{:S(2)}, u32[]{:S(2)}) async-start(f32[4,1,384]{2,1,0:T(1,128)} %reshape.199), calls=%async_computation.3 | async-start | bytes 12288 | tf_op jit(solution)/shard_map/all_to_all | solution.py:32
  152.0 32.9 %all-to-all-start.4 = ((f32[64,1,192]{2,1,0:T(1,128)}), f32[64,1,192]{2,1,0:T(1,128)S(1)}, u32[]{:S(2)}, u32[]{:S(2)}) async-start(f32[64,1,192]{2,1,0:T(1,128)} %reshape.201), calls=%async_computation.4 | async-start | bytes 131072 | tf_op jit(solution)/shard_map/all_to_all | solution.py:32
  198.0 31.2 %all-to-all-start.5 = ((f32[64,1,192]{2,1,0:T(1,128)}), f32[64,1,192]{2,1,0:T(1,128)S(1)}, u32[]{:S(2)}, u32[]{:S(2)}) async-start(f32[64,1,192]{2,1,0:T(1,128)} %reshape.203), calls=%async_computation.5 | async-start | bytes 131072 | tf_op jit(solution)/shard_map/all_to_all | solution.py:48
where the time goes:
time: 242 us; the launch traced here: 239 us
  waiting for transfers between devices  98.8 us (41%)
  starting transfers between devices  76.7 us (32%)
  other arithmetic  30.9 us (13%)
  local copies, waits for them, and re-layouts  16.4 us (7%)
  blocking collectives  14.5 us (6%)
    all_to_all x4, starting transfers between devices, sent_to_all(): return lax.all_to_all(copies, axis, split_axis=0, concat_axis=0, tiled=True)  64.6 us
    all_to_all x4, waiting for transfers between devices, sent_to_all(): return lax.all_to_all(copies, axis, split_axis=0, concat_axis=0, tiled=True)  52.4 us
    all_to_all x2, waiting for transfers between devices, sum_at_owner(): lax.all_to_all(in_blocks(value, dim, length), axis, 0, 0, tiled=True)  46.4 us
    all_to_all x2, starting transfers between devices, sum_at_owner(): lax.all_to_all(in_blocks(value, dim, length), axis, 0, 0, tiled=True)  12.2 us
    reduce_sum x8, other arithmetic, pair_block(): acceleration = jnp.sum(weight[None] * delta_pos, axis=2)  11 us
    unnamed x1, blocking collectives  7.96 us
    all_to_all x1, blocking collectives, sent_to_all(): return lax.all_to_all(copies, axis, split_axis=0, concat_axis=0, tiled=True)  6.53 us
    mul x8, other arithmetic, pair_block(): radial[None] * delta_pos  6.48 us
  transfers between devices with their start and end apart: 6, of which 5 were waited for; matrix products, arithmetic and copies ran while one was open for 8% of the time, Pallas kernels for 0%

commit v1 on v0

v1 whole, which is shorter than its diff:
```python
import functools

import jax
import jax.numpy as jnp
from jax import lax
from jax.experimental import pallas as pl
from jax.experimental.pallas import tpu as pltpu
from jax.sharding import PartitionSpec as P

LEVELS = 5
STEPS = 2
SPAN = 8

soften_sq = 0.0004
fine_step = 0.03125
MESH = pl.DeviceIdType.MESH
HIGHEST = lax.Precision.HIGHEST


def predict(pos, vel, acc, jerk, interval):
    new_pos = pos + interval * (vel + interval * (0.5 * acc + interval * jerk / 6.0))
    new_vel = vel + interval * (acc + 0.5 * interval * jerk)
    return new_pos, new_vel


def correct(acc_old, jerk_old, acc_new, jerk_new, pos_pred, vel_pred):
    snap_term = (-6.0 * (acc_old - acc_new) - fine_step * (4.0 * jerk_old + 2.0 * jerk_new)) / (
        fine_step * fine_step
    )
    crackle = (12.0 * (acc_old - acc_new) + 6.0 * fine_step * (jerk_old + jerk_new)) / (
        fine_step * fine_step * fine_step
    )
    pos = pos_pred + fine_step**4 / 24.0 * snap_term + fine_step**5 / 120.0 * crackle
    vel = vel_pred + fine_step**3 / 6.0 * snap_term + fine_step**4 / 24.0 * crackle
    return pos, vel


def spread(tile, wide):
    stars = tile.shape[1]
    columns = jnp.transpose(tile)
    for row in range(7):
        wide[row, 0:stars, :] = jnp.broadcast_to(columns[:, row : row + 1], (stars, 128))


def accumulate(wide, begin, count, targets, sums, pair, first):
    aim = [
        [jnp.broadcast_to(targets[2 * pair + i, row : row + 1, :], (8, 128)) for row in range(6)]
        for i in range(2)
    ]

    def body(step, totals):
        rows = pl.ds(pl.multiple_of(begin + step * 8, 8), 8)
        source = [wide[row, rows, :] for row in range(7)]
        finished = []
        for i in range(2):
            dx, dy, dz, du, dv, dw = [source[row] - aim[i][row] for row in range(6)]
            dist_sq = dx * dx + dy * dy + dz * dz + soften_sq
            inverse = lax.rsqrt(dist_sq)
            inv_sq = inverse * inverse
            weight = source[6] * inverse * inv_sq
            radial = (dx * du + dy * dv + dz * dw) * inv_sq * 3.0
            part = [weight * d for d in (dx, dy, dz)]
            part += [weight * (e - radial * d) for d, e in ((dx, du), (dy, dv), (dz, dw))]
            finished += part
        return tuple(t + p for t, p in zip(totals, finished))

    if first:
        totals = tuple(jnp.zeros((8, 128), jnp.float32) for _ in range(12))
    else:
        totals = tuple(sums[2 * pair + i, row] for i in range(2) for row in range(6))
    totals = lax.fori_loop(0, count // 8, body, totals, unroll=2)
    for i in range(2):
        for row in range(6):
            sums[2 * pair + i, row] = totals[6 * i + row]


def kernel(
    n_src,
    n_act,
    state_ref,
    mass_ref,
    phase_ref,
    level_ref,
    out_ref,
    own0,
    own1,
    tile_a,
    tile_b,
    got0,
    got1,
    got_act,
    aim0,
    aim1,
    wide,
    sums,
    give0,
    give1,
    take0,
    take1,
    line0,
    line1,
    lines0,
    lines1,
    hot,
    held,
    send_sem,
    recv_sem,
):
    n_col = n_src // SPAN
    me = lax.axis_index("src")
    act = lax.axis_index("act")
    place = lax.rem(me, SPAN)
    base = me - place
    stars = state_ref.shape[1]
    part = stars // n_act
    slots = hot.shape[0]

    col_peer = [{"src": lax.rem(me + SPAN * q, n_src), "act": act} for q in range(n_col)]
    row_peer = [{"src": base + lax.rem(place + r, SPAN), "act": act} for r in range(SPAN)]
    act_peer = [{"src": me, "act": lax.rem(act + i, n_act)} for i in range(n_act)]

    barrier = pltpu.get_barrier_semaphore()
    everyone = col_peer[1:] + row_peer[1:] + act_peer[1:]
    for peer in everyone:
        pl.semaphore_signal(barrier, inc=1, device_id=peer, device_id_type=MESH)

    counter = [0]

    def exchange(peers, source, target, rows=8):
        n = len(peers)
        copies = [None] * n
        for k in range(1, n):
            copies[n - k] = pltpu.make_async_remote_copy(
                src_ref=source(k),
                dst_ref=target.at[n - k, 0:rows],
                send_sem=send_sem.at[counter[0] + k],
                recv_sem=recv_sem.at[counter[0] + n - k],
                device_id=peers[k],
                device_id_type=MESH,
            )
        counter[0] += n
        return copies

    total = jnp.float32(stars * n_src)
    mine = pl.ds(pl.multiple_of(act * part, part), part)
    level = level_ref[:, mine]
    tick_count = jnp.left_shift(jnp.int32(1), LEVELS - 1 - level).astype(jnp.float32)
    weight = mass_ref[:, mine] / total
    for substep, own in ((0, own0), (1, own1)):
        elapsed = (
            jnp.where(
                level == LEVELS - 1,
                1.0,
                phase_ref[:, mine] * (tick_count - STEPS) + (substep + 1),
            )
            * fine_step
        )
        pos, vel = predict(
            state_ref[0:3, mine],
            state_ref[3:6, mine],
            state_ref[6:9, mine],
            state_ref[9:12, mine],
            elapsed,
        )
        own[0:3, :] = pos
        own[3:6, :] = vel
        own[6:7, :] = weight if substep == 0 else jnp.where(level == LEVELS - 1, 0.0, weight)
        own[7:8, :] = jnp.zeros((1, part), jnp.float32)

    is_active = level_ref[...] == LEVELS - 1
    flags = jnp.broadcast_to(jnp.where(is_active, 1.0, 0.0), (8, stars))
    before = lax.broadcasted_iota(jnp.int32, (stars, stars), 0) < lax.broadcasted_iota(
        jnp.int32, (stars, stars), 1
    )
    rank = jnp.dot(
        flags.astype(jnp.bfloat16),
        jnp.where(before, 1.0, 0.0).astype(jnp.bfloat16),
        preferred_element_type=jnp.float32,
    )[0:1, :]
    rank = jnp.where(is_active, rank, float(slots)).astype(jnp.int32)
    hot[...] = jnp.where(
        lax.broadcasted_iota(jnp.int32, (slots, stars), 0) == rank, 1.0, 0.0
    )
    over_stars = (((1,), (1,)), ((), ()))
    held[0:12, :] = lax.dot_general(
        state_ref[...], hot[...], over_stars, precision=HIGHEST, preferred_element_type=jnp.float32
    )
    held_mass = lax.dot_general(
        jnp.broadcast_to(mass_ref[...] / total, (8, stars)),
        hot[...],
        over_stars,
        precision=HIGHEST,
        preferred_element_type=jnp.float32,
    )[0:1, :]

    def predict_held(tile):
        pos, vel = predict(
            held[0:3, :], held[3:6, :], held[6:9, :], held[9:12, :], fine_step
        )
        tile[0:3, :] = pos
        tile[3:6, :] = vel
        tile[6:7, :] = held_mass
        tile[7:8, :] = jnp.zeros((1, slots), jnp.float32)

    predict_held(tile_a)
    aim0[0] = tile_a[...]
    spread(own0[...], wide)

    pl.semaphore_wait(barrier, len(everyone))
    cols0 = exchange(col_peer, lambda k: own0, got0)
    rows0 = exchange(row_peer, lambda k: tile_a, aim0)
    order = sorted(range(1, n_col), key=lambda q: -min(q, n_col - q))
    for q in order:
        cols0[q].start()
    for copy in rows0[1:]:
        copy.start()
    cols1 = exchange(col_peer, lambda k: own1, got1)

    def over_pairs(begin, count, targets, first):
        def one(pair, carry):
            accumulate(wide, begin, count, targets, sums, pair, first)
            return carry

        lax.fori_loop(0, SPAN // 2, one, 0)

    def last_block(begin, count, targets, give, copies):
        for pair in reversed(range(SPAN // 2)):
            accumulate(wide, begin, count, targets, sums, pair, False)
            for k in (2 * pair, 2 * pair + 1):
                for row in range(6):
                    give[k, row : row + 1, :] = jnp.sum(sums[k, row], axis=0, keepdims=True)
                if k > 0:
                    copies[SPAN - k].start()

    def reduced(give, take, copies, line, lines, act_copies):
        for copy in copies[1:]:
            copy.wait_recv()
        summed = give[0, 0:6, :]
        for r in range(1, SPAN):
            summed = summed + take[r, 0:6, :]
        line[0:6, :] = summed
        for copy in act_copies[1:]:
            copy.start()
        for copy in act_copies[1:]:
            copy.wait_recv()
        near = [summed] + [lines[i, 0:6, :] for i in range(1, n_act)]
        while len(near) > 1:
            half = len(near) // 2
            near = [near[i] + near[i + half] for i in range(half)]
        return near[0]

    def corrected(forces, tile):
        acc_old, jerk_old = held[6:9, :], held[9:12, :]
        acc_new, jerk_new = forces[0:3, :], forces[3:6, :]
        pos, vel = correct(acc_old, jerk_old, acc_new, jerk_new, tile[0:3, :], tile[3:6, :])
        held[0:3, :] = pos
        held[3:6, :] = vel
        held[6:9, :] = acc_new
        held[9:12, :] = jerk_new

    for copy in rows0[1:]:
        copy.wait_recv()
    over_pairs(0, part, aim0, True)
    arrival = order[::-1]
    gives0 = exchange(row_peer, lambda k: give0.at[k, 0:6], take0, 6)
    acts0 = exchange(act_peer, lambda k: line0.at[0:6], lines0, 6)
    for n, q in enumerate(arrival):
        cols0[q].wait_recv()
        spread(got0[q], wide)
        if q != arrival[-1]:
            over_pairs(0, part, aim0, False)
        else:
            last_block(0, part, aim0, give0, gives0)
        if n == 1:
            for copy in cols1[1:]:
                copy.start()
    corrected(reduced(give0, take0, gives0, line0, lines0, acts0), tile_a)

    predict_held(tile_b)
    cols2 = exchange(col_peer, lambda k: tile_b, got_act)
    rows1 = exchange(row_peer, lambda k: tile_b, aim1)
    for copy in rows1[1:]:
        copy.start()
    for q in order:
        cols2[q].start()
    aim1[0] = tile_b[...]
    spread(own1[...], wide)
    for copy in rows1[1:]:
        copy.wait_recv()
    over_pairs(0, part, aim1, True)
    for q in arrival:
        cols1[q].wait_recv()
        spread(got1[q], wide)
        over_pairs(0, part, aim1, False)
    share = slots // n_act
    first_slot = act * share
    spread(tile_b[...], wide)
    over_pairs(first_slot, share, aim1, False)
    gives1 = exchange(row_peer, lambda k: give1.at[k, 0:6], take1, 6)
    acts1 = exchange(act_peer, lambda k: line1.at[0:6], lines1, 6)
    for q in arrival:
        cols2[q].wait_recv()
        spread(got_act[q], wide)
        if q != arrival[-1]:
            over_pairs(first_slot, share, aim1, False)
        else:
            last_block(first_slot, share, aim1, give1, gives1)
    corrected(reduced(give1, take1, gives1, line1, lines1, acts1), tile_b)

    moved = jnp.dot(held[...], hot[...], precision=HIGHEST, preferred_element_type=jnp.float32)
    out_ref[...] = jnp.where(is_active, moved[0:12, :], state_ref[...])
    for copies in (cols0, rows0, cols1, gives0, acts0, cols2, rows1, gives1, acts1):
        for copy in copies[1:]:
            copy.wait_send()


def solution(mesh):
    n_src, n_act = mesh.shape["src"], mesh.shape["act"]
    n_col = n_src // SPAN

    def per_device(star_state, masses, phases, levels, active_list, active_count):
        stars = star_state.shape[1]
        part = stars // n_act
        slots = 2 * active_list.shape[0]
        vmem = pl.BlockSpec(memory_space=pltpu.VMEM)
        n_sem = 3 * n_col + 4 * SPAN + 2 * n_act

        def tiles(*lead):
            return pltpu.VMEM((*lead, 8, 128), jnp.float32)

        return pl.pallas_call(
            functools.partial(kernel, n_src, n_act),
            out_shape=jax.ShapeDtypeStruct(star_state.shape, jnp.float32),
            in_specs=[vmem] * 4,
            out_specs=vmem,
            scratch_shapes=[
                pltpu.VMEM((8, part), jnp.float32),
                pltpu.VMEM((8, part), jnp.float32),
                pltpu.VMEM((8, slots), jnp.float32),
                pltpu.VMEM((8, slots), jnp.float32),
                pltpu.VMEM((n_col, 8, part), jnp.float32),
                pltpu.VMEM((n_col, 8, part), jnp.float32),
                pltpu.VMEM((n_col, 8, slots), jnp.float32),
                pltpu.VMEM((SPAN, 8, slots), jnp.float32),
                pltpu.VMEM((SPAN, 8, slots), jnp.float32),
                pltpu.VMEM((8, max(part, slots), 128), jnp.float32),
                tiles(SPAN, 6),
                tiles(SPAN),
                tiles(SPAN),
                tiles(SPAN),
                tiles(SPAN),
                tiles(),
                tiles(),
                tiles(n_act),
                tiles(n_act),
                pltpu.VMEM((slots, stars), jnp.float32),
                pltpu.VMEM((12, slots), jnp.float32),
                pltpu.SemaphoreType.DMA((n_sem,)),
                pltpu.SemaphoreType.DMA((n_sem,)),
            ],
            compiler_params=pltpu.CompilerParams(collective_id=0, has_side_effects=True),
        )(
            star_state,
            masses.reshape(1, stars),
            phases.reshape(1, stars),
            levels.reshape(1, stars),
        )

    in_specs = (
        P(None, ("groups", "src")),
        P(("groups", "src")),
        P(("groups", "src")),
        P(("groups", "src")),
        P(("groups", "src", "act")),
        P(("groups", "src", "act")),
    )
    return jax.shard_map(
        per_device,
        mesh=mesh,
        in_specs=in_specs,
        out_specs=P(None, ("groups", "src")),
        check_vma=False,
    )
```

time: 242 us -> 102 us (0.42)
  Pallas kernels: 0 us -> 100 us
  waiting for transfers between devices: 98.8 us -> 0 us
  starting transfers between devices: 76.7 us -> 0 us
  other arithmetic: 30.9 us -> 0 us
  local copies, waits for them, and re-layouts: 16.4 us -> 1.38 us
  blocking collectives: 14.5 us -> 0 us
    pallas_call x0 -> x1, Pallas kernels: none -> 100 us  [per_device(): pl.pallas_call(functools.partial(kernel, n_src, n_act), out_shape=jax.Sha...]
    all_to_all x6 -> x0, waiting for transfers between devices: 98.8 us -> none  [the longest x4 52.4 us: sent_to_all(): return lax.all_to_all(copies, axis, split_axis=0, concat_axis=0, tiled=True)]
    all_to_all x6 -> x0, starting transfers between devices: 76.7 us -> none  [the longest x4 64.6 us: sent_to_all(): return lax.all_to_all(copies, axis, split_axis=0, concat_axis=0, tiled=True)]
    reduce_sum x13 -> x0, other arithmetic: 11.5 us -> none  [the longest x8 11 us: pair_block(): acceleration = jnp.sum(weight[None] * delta_pos, axis=2)]
    unnamed x1 -> x0, blocking collectives: 7.96 us -> none
    mul x10 -> x0, other arithmetic: 7.19 us -> none  [the longest x8 6.48 us: pair_block(): radial[None] * delta_pos]
    all_to_all x1 -> x0, blocking collectives: 6.53 us -> none  [sent_to_all(): return lax.all_to_all(copies, axis, split_axis=0, concat_axis=0, tiled=True)]
    all_to_all x7 -> x0, other arithmetic: 4.98 us -> none  [the longest x5 3.45 us: sent_to_all(): return lax.all_to_all(copies, axis, split_axis=0, concat_axis=0, tiled=True)]
  transfers between devices with their start and end apart: 6 -> 0, of which waited for: 5 -> 0; matrix products, arithmetic and copies ran while one was open for 8% -> 0% of each run, Pallas kernels for 0% -> 0%
where the time goes in v1:
time: 102 us; the launch traced here: 101 us
  Pallas kernels  100 us (98%)
  local copies, waits for them, and re-layouts  1.38 us (1%)
    pallas_call x1, Pallas kernels, per_device(): pl.pallas_call(functools.partial(kernel, n_src, n_act), out_shape=jax.Sha...  100 us

profile of v1, /device:TPU:33, one launch (start us, length us, event | category | flops | bytes accessed | tf_op | source)
XLA Modules:
  0.0 101.4 jit_solution(16019273949930432265)
XLA Ops:
  0.0 100.0 %shard_map.46 = f32[12,512]{1,0:T(8,128)} custom-call(f32[12,512]{1,0:T(8,128)} %state_ref.1, f32[1,512]{1,0:T(1,128)} %bitcast.3, f32[1,512]{1,0:T(1,128)} %bitcast.4, s32[1,512]{1,0:T(1,128)} %bitcast.5), custom_call_target="tpu_custom_call" | custom-call | tf_op jit(solution)/shard_map/pallas_call | solution.py:331
  100.0 1.4 %copy.6 = f32[12,512]{1,0:T(8,128)} copy(f32[12,512]{1,0:T(8,128)} %shard_map.46) | data formatting | bytes 49152

commit v2 on v1

--- a/solution.py
+++ b/solution.py
@@ -42,14 +42,21 @@
         wide[row, 0:stars, :] = jnp.broadcast_to(columns[:, row : row + 1], (stars, 128))
 
 
-def accumulate(wide, begin, count, targets, sums, pair, first):
+def spread_part(tile, columns, begin, count, wide, at):
+    columns[...] = jnp.transpose(tile)
+    chosen = columns[pl.ds(pl.multiple_of(begin, count), count), :]
+    for row in range(7):
+        wide[row, at : at + count, :] = jnp.broadcast_to(chosen[:, row : row + 1], (count, 128))
+
+
+def accumulate(wide, count, targets, sums, pair, first):
     aim = [
         [jnp.broadcast_to(targets[2 * pair + i, row : row + 1, :], (8, 128)) for row in range(6)]
         for i in range(2)
     ]
 
     def body(step, totals):
-        rows = pl.ds(pl.multiple_of(begin + step * 8, 8), 8)
+        rows = pl.ds(pl.multiple_of(step * 8, 8), 8)
         source = [wide[row, rows, :] for row in range(7)]
         finished = []
         for i in range(2):
@@ -72,6 +79,15 @@
     for i in range(2):
         for row in range(6):
             sums[2 * pair + i, row] = totals[6 * i + row]
+
+
+def flipped(place, r):
+    result, bit = place, 1
+    while bit < SPAN:
+        if r & bit:
+            result = result + bit * (1 - 2 * lax.rem(place // bit, 2))
+        bit *= 2
+    return result
 
 
 def kernel(
@@ -92,6 +108,7 @@
     aim0,
     aim1,
     wide,
+    columns,
     sums,
     give0,
     give1,
@@ -105,41 +122,100 @@
     held,
     send_sem,
     recv_sem,
+    down_sem,
+    up_sem,
+    block_sem,
+    next_ready,
+    row_ready,
+    act_ready,
 ):
     n_col = n_src // SPAN
     me = lax.axis_index("src")
     act = lax.axis_index("act")
+    group = lax.axis_index("groups")
     place = lax.rem(me, SPAN)
+    col = me // SPAN
     base = me - place
     stars = state_ref.shape[1]
     part = stars // n_act
     slots = hot.shape[0]
 
+    col_shift = jnp.where((place == 0) & (act == 0) & (group == 0), 1, 0)
+    row_shift = jnp.where((col == 0) & (act == 0) & (group == 0), 1, 0)
+    act_shift = jnp.where((me == 0) & (group == 0), 1, 0)
+    order = lax.rem(col - col_shift + n_col, n_col)
+    row_order = lax.rem(place - row_shift + SPAN, SPAN)
+    act_order = lax.rem(act - act_shift + n_act, n_act)
+
+    def ordered(b):
+        return {"src": lax.rem(b + col_shift + n_col, n_col) * SPAN + place, "act": act}
+
     col_peer = [{"src": lax.rem(me + SPAN * q, n_src), "act": act} for q in range(n_col)]
-    row_peer = [{"src": base + lax.rem(place + r, SPAN), "act": act} for r in range(SPAN)]
-    act_peer = [{"src": me, "act": lax.rem(act + i, n_act)} for i in range(n_act)]
+    row_place = [flipped(place, r) for r in range(SPAN)]
+    row_peer = [{"src": base + p, "act": act} for p in row_place]
+    act_place = [lax.rem(act + i, n_act) for i in range(n_act)]
+    act_peer = [{"src": me, "act": a} for a in act_place]
+    row_later = [lax.rem(p - row_shift + SPAN, SPAN) > row_order for p in row_place]
+    act_later = [lax.rem(a - act_shift + n_act, n_act) > act_order for a in act_place]
+
+    def signal(semaphore, peer):
+        pl.semaphore_signal(semaphore, inc=1, device_id=peer, device_id_type=MESH)
 
     barrier = pltpu.get_barrier_semaphore()
-    everyone = col_peer[1:] + row_peer[1:] + act_peer[1:]
-    for peer in everyone:
-        pl.semaphore_signal(barrier, inc=1, device_id=peer, device_id_type=MESH)
+
+    def greet(b, carry):
+        signal(barrier, ordered(b))
+        return carry
+
+    lax.fori_loop(order + 1, n_col, greet, 0)
+    for later, peers in ((row_later, row_peer), (act_later, act_peer)):
+        for k in range(1, len(peers)):
+            pl.when(later[k])(functools.partial(signal, barrier, peers[k]))
 
     counter = [0]
 
-    def exchange(peers, source, target, rows=8):
+    def exchange(peers, source, target, back, rows=8):
         n = len(peers)
         copies = [None] * n
         for k in range(1, n):
-            copies[n - k] = pltpu.make_async_remote_copy(
+            copies[back(k)] = pltpu.make_async_remote_copy(
                 src_ref=source(k),
-                dst_ref=target.at[n - k, 0:rows],
+                dst_ref=target.at[back(k), 0:rows],
                 send_sem=send_sem.at[counter[0] + k],
-                recv_sem=recv_sem.at[counter[0] + n - k],
+                recv_sem=recv_sem.at[counter[0] + back(k)],
                 device_id=peers[k],
                 device_id_type=MESH,
             )
         counter[0] += n
         return copies
+
+    def col_back(k):
+        return n_col - k
+
+    def row_back(k):
+        return k
+
+    def act_back(k):
+        return n_act - k
+
+    def block_copy(source, b, semaphore, peer):
+        return pltpu.make_async_remote_copy(
+            src_ref=source,
+            dst_ref=got0.at[b],
+            send_sem=semaphore,
+            recv_sem=block_sem.at[b],
+            device_id=peer,
+            device_id_type=MESH,
+        )
+
+    def down(b):
+        return block_copy(own0, order, down_sem.at[b], ordered(b))
+
+    def up():
+        return block_copy(own0, order, up_sem.at[order], ordered(order + 1))
+
+    def pass_up(b):
+        return block_copy(got0.at[b], b, up_sem.at[b], ordered(order + 1))
 
     total = jnp.float32(stars * n_src)
     mine = pl.ds(pl.multiple_of(act * part, part), part)
@@ -204,35 +280,51 @@
 
     predict_held(tile_a)
     aim0[0] = tile_a[...]
-    spread(own0[...], wide)
-
-    pl.semaphore_wait(barrier, len(everyone))
-    cols0 = exchange(col_peer, lambda k: own0, got0)
-    rows0 = exchange(row_peer, lambda k: tile_a, aim0)
-    order = sorted(range(1, n_col), key=lambda q: -min(q, n_col - q))
-    for q in order:
-        cols0[q].start()
-    for copy in rows0[1:]:
-        copy.start()
-    cols1 = exchange(col_peer, lambda k: own1, got1)
-
-    def over_pairs(begin, count, targets, first):
+
+    earlier = order + row_order + act_order
+    pl.when(earlier > 0)(lambda: pl.semaphore_wait(barrier, earlier))
+    rows0 = exchange(row_peer, lambda k: tile_a, aim0, row_back)
+    pl.when(order > 0)(lambda: signal(next_ready, ordered(order - 1)))
+    for r in range(1, SPAN):
+        pl.when(~row_later[r])(functools.partial(signal, row_ready.at[r], row_peer[r]))
+    for i in range(1, n_act):
+        pl.when(~act_later[i])(functools.partial(signal, act_ready.at[n_act - i], act_peer[i]))
+    far_first = sorted(range(1, n_col), key=lambda q: -min(q, n_col - q))
+    near_first = far_first[::-1]
+    for q in far_first:
+        pl.when(order >= q)(lambda q=q: down(order - q).start())
+    for r in range(1, SPAN):
+        pl.when(~row_later[r])(lambda r=r: rows0[r].start())
+    spread(own0[...], wide.at[0])
+    for r in range(1, SPAN):
+
+        @pl.when(row_later[r])
+        def _(r=r):
+            pl.semaphore_wait(row_ready.at[r], 1)
+            rows0[r].start()
+
+    @pl.when(order < n_col - 1)
+    def _():
+        pl.semaphore_wait(next_ready, 1)
+        up().start()
+
+    def over_pairs(source, count, targets, first, lowest=0):
         def one(pair, carry):
-            accumulate(wide, begin, count, targets, sums, pair, first)
+            accumulate(source, count, targets, sums, pair, first)
             return carry
 
-        lax.fori_loop(0, SPAN // 2, one, 0)
-
-    def last_block(begin, count, targets, give, copies):
+        lax.fori_loop(lowest, SPAN // 2, one, 0)
+
+    def last_block(source, count, targets, give, copies):
         for pair in reversed(range(SPAN // 2)):
-            accumulate(wide, begin, count, targets, sums, pair, False)
+            accumulate(source, count, targets, sums, pair, False)
             for k in (2 * pair, 2 * pair + 1):
                 for row in range(6):
                     give[k, row : row + 1, :] = jnp.sum(sums[k, row], axis=0, keepdims=True)
                 if k > 0:
-                    copies[SPAN - k].start()
-
-    def reduced(give, take, copies, line, lines, act_copies):
+                    copies[k].start()
+
+    def reduced(give, take, copies, line, lines, act_copies, meet):
         for copy in copies[1:]:
             copy.wait_recv()
         summed = give[0, 0:6, :]
@@ -241,6 +333,7 @@
         line[0:6, :] = summed
         for copy in act_copies[1:]:
             copy.start()
+        meet()
         for copy in act_copies[1:]:
             copy.wait_recv()
         near = [summed] + [lines[i, 0:6, :] for i in range(1, n_act)]
@@ -258,60 +351,113 @@
         held[6:9, :] = acc_new
         held[9:12, :] = jerk_new
 
+    def wait_block(b):
+        block_copy(own0, b, down_sem.at[b], ordered(order + 1)).wait_recv()
+
     for copy in rows0[1:]:
         copy.wait_recv()
-    over_pairs(0, part, aim0, True)
-    arrival = order[::-1]
-    gives0 = exchange(row_peer, lambda k: give0.at[k, 0:6], take0, 6)
-    acts0 = exchange(act_peer, lambda k: line0.at[0:6], lines0, 6)
-    for n, q in enumerate(arrival):
-        cols0[q].wait_recv()
-        spread(got0[q], wide)
-        if q != arrival[-1]:
-            over_pairs(0, part, aim0, False)
-        else:
-            last_block(0, part, aim0, give0, gives0)
-        if n == 1:
-            for copy in cols1[1:]:
-                copy.start()
-    corrected(reduced(give0, take0, gives0, line0, lines0, acts0), tile_a)
+    over_pairs(wide.at[0], part, aim0, True)
+
+    @pl.when(order < n_col - 1)
+    def _():
+        def forward(j, carry):
+            wait_block(order - j)
+            pass_up(order - j).start()
+            return carry
+
+        lax.fori_loop(1, order + 1, forward, 0)
+
+    def lower(j, carry):
+        pl.when(order == n_col - 1)(lambda: wait_block(order - j))
+        spread(got0[order - j], wide.at[0])
+        over_pairs(wide.at[0], part, aim0, False)
+        return carry
+
+    lax.fori_loop(1, jnp.minimum(order, n_col - 2) + 1, lower, 0)
+
+    def upper(b, carry):
+        wait_block(b)
+        spread(got0[b], wide.at[0])
+        over_pairs(wide.at[0], part, aim0, False)
+        return carry
+
+    lax.fori_loop(order + 1, n_col - 1, upper, 0)
+    for i in range(1, n_act):
+        pl.when(act_later[i])(lambda i=i: pl.semaphore_wait(act_ready.at[i], 1))
+    gives0 = exchange(row_peer, lambda k: give0.at[k, 0:6], take0, row_back, 6)
+    acts0 = exchange(act_peer, lambda k: line0.at[0:6], lines0, act_back, 6)
+    cols1 = exchange(col_peer, lambda k: own1, got1, col_back)
+    final = jnp.where(order == n_col - 1, 0, n_col - 1)
+    wait_block(final)
+    spread(got0[final], wide.at[0])
+    last_block(wide.at[0], part, aim0, give0, gives0)
+
+    def send_second():
+        for q in far_first:
+            cols1[n_col - q].start()
+        spread(own1[...], wide.at[0])
+
+    corrected(reduced(give0, take0, gives0, line0, lines0, acts0, send_second), tile_a)
 
     predict_held(tile_b)
-    cols2 = exchange(col_peer, lambda k: tile_b, got_act)
-    rows1 = exchange(row_peer, lambda k: tile_b, aim1)
+    cols2 = exchange(col_peer, lambda k: tile_b, got_act, col_back)
+    rows1 = exchange(row_peer, lambda k: tile_b, aim1, row_back)
+    cols2[n_col - far_first[0]].start()
     for copy in rows1[1:]:
         copy.start()
-    for q in order:
-        cols2[q].start()
+    for q in far_first[1:]:
+        cols2[n_col - q].start()
     aim1[0] = tile_b[...]
-    spread(own1[...], wide)
-    for copy in rows1[1:]:
-        copy.wait_recv()
-    over_pairs(0, part, aim1, True)
-    for q in arrival:
-        cols1[q].wait_recv()
-        spread(got1[q], wide)
-        over_pairs(0, part, aim1, False)
     share = slots // n_act
     first_slot = act * share
-    spread(tile_b[...], wide)
-    over_pairs(first_slot, share, aim1, False)
-    gives1 = exchange(row_peer, lambda k: give1.at[k, 0:6], take1, 6)
-    acts1 = exchange(act_peer, lambda k: line1.at[0:6], lines1, 6)
-    for q in arrival:
+    spread_part(tile_b[...], columns, first_slot, share, wide.at[1], 0)
+    rows1[1].wait_recv()
+    accumulate(wide.at[0], part, aim1, sums, 0, True)
+    for n, q in enumerate(near_first[:2]):
+        cols1[q].wait_recv()
+        spread(got1[q], wide.at[2 + n])
+        accumulate(wide.at[2 + n], part, aim1, sums, 0, False)
+    for copy in rows1[2:]:
+        copy.wait_recv()
+    over_pairs(wide.at[0], part, aim1, True, 1)
+    over_pairs(wide.at[2], part, aim1, False, 1)
+    over_pairs(wide.at[3], part, aim1, False, 1)
+    for q in near_first[2:]:
+        cols1[q].wait_recv()
+        spread(got1[q], wide.at[0])
+        over_pairs(wide.at[0], part, aim1, False)
+    gives1 = exchange(row_peer, lambda k: give1.at[k, 0:6], take1, row_back, 6)
+    acts1 = exchange(act_peer, lambda k: line1.at[0:6], lines1, act_back, 6)
+    for n, q in enumerate(near_first[:-1]):
         cols2[q].wait_recv()
-        spread(got_act[q], wide)
-        if q != arrival[-1]:
-            over_pairs(first_slot, share, aim1, False)
-        else:
-            last_block(first_slot, share, aim1, give1, gives1)
-    corrected(reduced(give1, take1, gives1, line1, lines1, acts1), tile_b)
+        spread_part(got_act[q], columns, first_slot, share, wide.at[1], (n + 1) * share)
+    over_pairs(wide.at[1], (n_col - 1) * share, aim1, False)
+    cols2[near_first[-1]].wait_recv()
+    spread_part(got_act[near_first[-1]], columns, first_slot, share, wide.at[2], 0)
+    last_block(wide.at[2], share, aim1, give1, gives1)
+    corrected(reduced(give1, take1, gives1, line1, lines1, acts1, lambda: None), tile_b)
 
     moved = jnp.dot(held[...], hot[...], precision=HIGHEST, preferred_element_type=jnp.float32)
     out_ref[...] = jnp.where(is_active, moved[0:12, :], state_ref[...])
-    for copies in (cols0, rows0, cols1, gives0, acts0, cols2, rows1, gives1, acts1):
+    for copies in (rows0, cols1, gives0, acts0, cols2, rows1, gives1, acts1):
         for copy in copies[1:]:
             copy.wait_send()
+
+    def down_sent(b, carry):
+        down(b).wait_send()
+        return carry
+
+    lax.fori_loop(0, order, down_sent, 0)
+
+    @pl.when(order < n_col - 1)
+    def _():
+        up().wait_send()
+
+        def up_sent(b, carry):
+            pass_up(b).wait_send()
+            return carry
+
+        lax.fori_loop(0, order, up_sent, 0)
 
 
 def solution(mesh):
@@ -323,7 +469,7 @@
         part = stars // n_act
         slots = 2 * active_list.shape[0]
         vmem = pl.BlockSpec(memory_space=pltpu.VMEM)
-        n_sem = 3 * n_col + 4 * SPAN + 2 * n_act
+        n_sem = 2 * n_col + 4 * SPAN + 2 * n_act
 
         def tiles(*lead):
             return pltpu.VMEM((*lead, 8, 128), jnp.float32)
@@ -343,7 +489,8 @@
                 pltpu.VMEM((n_col, 8, slots), jnp.float32),
                 pltpu.VMEM((SPAN, 8, slots), jnp.float32),
                 pltpu.VMEM((SPAN, 8, slots), jnp.float32),
-                pltpu.VMEM((8, max(part, slots), 128), jnp.float32),
+                pltpu.VMEM((4, 7, max(part, n_col * slots // n_act), 128), jnp.float32),
+                pltpu.VMEM((slots, 8), jnp.float32),
                 tiles(SPAN, 6),
                 tiles(SPAN),
                 tiles(SPAN),
@@ -357,6 +504,12 @@
                 pltpu.VMEM((12, slots), jnp.float32),
                 pltpu.SemaphoreType.DMA((n_sem,)),
                 pltpu.SemaphoreType.DMA((n_sem,)),
+                pltpu.SemaphoreType.DMA((n_col,)),
+                pltpu.SemaphoreType.DMA((n_col,)),
+                pltpu.SemaphoreType.DMA((n_col,)),
+                pltpu.SemaphoreType.REGULAR,
+                pltpu.SemaphoreType.REGULAR((SPAN,)),
+                pltpu.SemaphoreType.REGULAR((n_act,)),
             ],
             compiler_params=pltpu.CompilerParams(collective_id=0, has_side_effects=True),
         )(

time: 102 us -> 113 us (1.11)
  Pallas kernels: 100 us -> 110 us
    pallas_call x1, Pallas kernels: 100 us -> 110 us  [per_device(): pl.pallas_call(functools.partial(kernel, n_src, n_act), out_shape=jax.Sha...]
where the time goes in v2:
time: 113 us; the launch traced here: 112 us
  Pallas kernels  110 us (97%)
  local copies, waits for them, and re-layouts  1.38 us (1%)
    pallas_call x1, Pallas kernels, per_device(): pl.pallas_call(functools.partial(kernel, n_src, n_act), out_shape=jax.Sha...  110 us

profile of v2, /device:TPU:33, one launch (start us, length us, event | category | flops | bytes accessed | tf_op | source)
XLA Modules:
  0.0 111.8 jit_solution(15454073655636344450)
XLA Ops:
  0.0 110.4 %shard_map.46 = f32[12,512]{1,0:T(8,128)} custom-call(f32[12,512]{1,0:T(8,128)} %state_ref.1, f32[1,512]{1,0:T(1,128)} %bitcast.3, f32[1,512]{1,0:T(1,128)} %bitcast.4, s32[1,512]{1,0:T(1,128)} %bitcast.5), custom_call_target="tpu_custom_call" | custom-call | tf_op jit(solution)/shard_map/pallas_call | solution.py:477
  110.4 1.4 %copy.6 = f32[12,512]{1,0:T(8,128)} copy(f32[12,512]{1,0:T(8,128)} %shard_map.46) | data formatting | bytes 49152

commit v3 on v2

--- a/solution.py
+++ b/solution.py
@@ -93,11 +93,16 @@
 def kernel(
     n_src,
     n_act,
+    state_in,
+    mass_in,
+    phase_in,
+    level_in,
+    out_ref,
     state_ref,
     mass_ref,
     phase_ref,
     level_ref,
-    out_ref,
+    in_sem,
     own0,
     own1,
     tile_a,
@@ -129,6 +134,19 @@
     row_ready,
     act_ready,
 ):
+    loads = [
+        pltpu.make_async_copy(source, target, in_sem.at[k])
+        for k, (source, target) in enumerate(
+            (
+                (state_in, state_ref),
+                (mass_in, mass_ref),
+                (phase_in, phase_ref),
+                (level_in, level_ref),
+            )
+        )
+    ]
+    for load in loads:
+        load.start()
     n_col = n_src // SPAN
     me = lax.axis_index("src")
     act = lax.axis_index("act")
@@ -217,12 +235,24 @@
     def pass_up(b):
         return block_copy(got0.at[b], b, up_sem.at[b], ordered(order + 1))
 
+    earlier = order + row_order + act_order
+    pl.when(earlier > 0)(lambda: pl.semaphore_wait(barrier, earlier))
+    rows0 = exchange(row_peer, lambda k: tile_a, aim0, row_back)
+    pl.when(order > 0)(lambda: signal(next_ready, ordered(order - 1)))
+    for r in range(1, SPAN):
+        pl.when(~row_later[r])(functools.partial(signal, row_ready.at[r], row_peer[r]))
+    for i in range(1, n_act):
+        pl.when(~act_later[i])(functools.partial(signal, act_ready.at[n_act - i], act_peer[i]))
+
+    for load in loads:
+        load.wait()
     total = jnp.float32(stars * n_src)
     mine = pl.ds(pl.multiple_of(act * part, part), part)
     level = level_ref[:, mine]
     tick_count = jnp.left_shift(jnp.int32(1), LEVELS - 1 - level).astype(jnp.float32)
     weight = mass_ref[:, mine] / total
-    for substep, own in ((0, own0), (1, own1)):
+
+    def predict_own(substep, own):
         elapsed = (
             jnp.where(
                 level == LEVELS - 1,
@@ -243,6 +273,13 @@
         own[6:7, :] = weight if substep == 0 else jnp.where(level == LEVELS - 1, 0.0, weight)
         own[7:8, :] = jnp.zeros((1, part), jnp.float32)
 
+    predict_own(0, own0)
+    far_first = sorted(range(1, n_col), key=lambda q: -min(q, n_col - q))
+    near_first = far_first[::-1]
+    for q in far_first:
+        pl.when(order >= q)(lambda q=q: down(order - q).start())
+
+    predict_own(1, own1)
     is_active = level_ref[...] == LEVELS - 1
     flags = jnp.broadcast_to(jnp.where(is_active, 1.0, 0.0), (8, stars))
     before = lax.broadcasted_iota(jnp.int32, (stars, stars), 0) < lax.broadcasted_iota(
@@ -281,32 +318,25 @@
     predict_held(tile_a)
     aim0[0] = tile_a[...]
 
-    earlier = order + row_order + act_order
-    pl.when(earlier > 0)(lambda: pl.semaphore_wait(barrier, earlier))
-    rows0 = exchange(row_peer, lambda k: tile_a, aim0, row_back)
-    pl.when(order > 0)(lambda: signal(next_ready, ordered(order - 1)))
-    for r in range(1, SPAN):
-        pl.when(~row_later[r])(functools.partial(signal, row_ready.at[r], row_peer[r]))
-    for i in range(1, n_act):
-        pl.when(~act_later[i])(functools.partial(signal, act_ready.at[n_act - i], act_peer[i]))
-    far_first = sorted(range(1, n_col), key=lambda q: -min(q, n_col - q))
-    near_first = far_first[::-1]
-    for q in far_first:
-        pl.when(order >= q)(lambda q=q: down(order - q).start())
     for r in range(1, SPAN):
         pl.when(~row_later[r])(lambda r=r: rows0[r].start())
     spread(own0[...], wide.at[0])
-    for r in range(1, SPAN):
-
-        @pl.when(row_later[r])
-        def _(r=r):
-            pl.semaphore_wait(row_ready.at[r], 1)
-            rows0[r].start()
+    def answer_row():
+        for r in range(1, SPAN):
+
+            @pl.when(row_later[r])
+            def _(r=r):
+                pl.semaphore_wait(row_ready.at[r], 1)
+                rows0[r].start()
+
+    pl.when(row_shift == 0)(answer_row)
 
     @pl.when(order < n_col - 1)
     def _():
         pl.semaphore_wait(next_ready, 1)
         up().start()
+
+    pl.when(row_shift == 1)(answer_row)
 
     def over_pairs(source, count, targets, first, lowest=0):
         def one(pair, carry):
@@ -477,9 +507,14 @@
         return pl.pallas_call(
             functools.partial(kernel, n_src, n_act),
             out_shape=jax.ShapeDtypeStruct(star_state.shape, jnp.float32),
-            in_specs=[vmem] * 4,
+            in_specs=[pl.BlockSpec(memory_space=pl.ANY)] * 4,
             out_specs=vmem,
             scratch_shapes=[
+                pltpu.VMEM(star_state.shape, jnp.float32),
+                pltpu.VMEM((1, stars), jnp.float32),
+                pltpu.VMEM((1, stars), jnp.float32),
+                pltpu.VMEM((1, stars), jnp.int32),
+                pltpu.SemaphoreType.DMA((4,)),
                 pltpu.VMEM((8, part), jnp.float32),
                 pltpu.VMEM((8, part), jnp.float32),
                 pltpu.VMEM((8, slots), jnp.float32),

time: 113 us -> 94.2 us (0.83)
  Pallas kernels: 110 us -> 92.5 us
    pallas_call x1, Pallas kernels: 110 us -> 92.5 us  [per_device(): pl.pallas_call(functools.partial(kernel, n_src, n_act), out_shape=jax.Sha...]
where the time goes in v3:
time: 94.2 us; the launch traced here: 93.9 us
  Pallas kernels  92.5 us (98%)
  local copies, waits for them, and re-layouts  1.38 us (1%)
    pallas_call x1, Pallas kernels, per_device(): pl.pallas_call(functools.partial(kernel, n_src, n_act), out_shape=jax.Sha...  92.5 us

profile of v3, /device:TPU:33, one launch (start us, length us, event | category | flops | bytes accessed | tf_op | source)
XLA Modules:
  0.0 93.9 jit_solution(253469648729946762)
XLA Ops:
  0.0 92.5 %shard_map.46 = f32[12,512]{1,0:T(8,128)} custom-call(f32[12,512]{1,0:T(8,128)} %state_in.1, f32[1,512]{1,0:T(1,128)} %bitcast.3, f32[1,512]{1,0:T(1,128)} %bitcast.4, s32[1,512]{1,0:T(1,128)} %bitcast.5), custom_call_target="tpu_custom_call" | custom-call | tf_op jit(solution)/shard_map/pallas_call | solution.py:507
  92.6 1.4 %copy.6 = f32[12,512]{1,0:T(8,128)} copy(f32[12,512]{1,0:T(8,128)} %shard_map.46) | data formatting | bytes 49152

commit v4 on v3

--- a/solution.py
+++ b/solution.py
@@ -133,6 +133,8 @@
     next_ready,
     row_ready,
     act_ready,
+    wrap_sem,
+    wrap_ready,
 ):
     loads = [
         pltpu.make_async_copy(source, target, in_sem.at[k])
@@ -239,6 +241,8 @@
     pl.when(earlier > 0)(lambda: pl.semaphore_wait(barrier, earlier))
     rows0 = exchange(row_peer, lambda k: tile_a, aim0, row_back)
     pl.when(order > 0)(lambda: signal(next_ready, ordered(order - 1)))
+    for t in range(2):
+        pl.when(order == n_col - 2 + t)(lambda t=t: signal(wrap_ready.at[t], ordered(0)))
     for r in range(1, SPAN):
         pl.when(~row_later[r])(functools.partial(signal, row_ready.at[r], row_peer[r]))
     for i in range(1, n_act):
@@ -384,6 +388,31 @@
     def wait_block(b):
         block_copy(own0, b, down_sem.at[b], ordered(order + 1)).wait_recv()
 
+    half = n_col // 2
+
+    def cut(o):
+        return jnp.where(o >= n_col - 2, o - half + 1, 0)
+
+    is_last = order == n_col - 1
+    passed = jnp.where(is_last, 0, order - cut(order + 1))
+
+    def wraps(t):
+        return [
+            block_copy(
+                own0 if b == 0 else got0.at[b], b, wrap_sem.at[t, b], ordered(n_col - 2 + t)
+            )
+            for b in range(half - 1 + t)
+        ]
+
+    @pl.when(order == 0)
+    def _():
+        for b in range(1, half):
+            wait_block(b)
+        for t in range(2):
+            pl.semaphore_wait(wrap_ready.at[t], 1)
+            for copy in wraps(t):
+                copy.start()
+
     for copy in rows0[1:]:
         copy.wait_recv()
     over_pairs(wide.at[0], part, aim0, True)
@@ -395,29 +424,40 @@
             pass_up(order - j).start()
             return carry
 
-        lax.fori_loop(1, order + 1, forward, 0)
-
-    def lower(j, carry):
-        pl.when(order == n_col - 1)(lambda: wait_block(order - j))
-        spread(got0[order - j], wide.at[0])
-        over_pairs(wide.at[0], part, aim0, False)
-        return carry
-
-    lax.fori_loop(1, jnp.minimum(order, n_col - 2) + 1, lower, 0)
-
-    def upper(b, carry):
-        wait_block(b)
+        lax.fori_loop(1, passed + 1, forward, 0)
+
+    def pull(b):
         spread(got0[b], wide.at[0])
         over_pairs(wide.at[0], part, aim0, False)
+
+    def lower(j, carry):
+        pl.when(j > passed)(lambda: wait_block(order - j))
+        pull(order - j)
         return carry
 
-    lax.fori_loop(order + 1, n_col - 1, upper, 0)
+    def upper(b, carry):
+        pl.when((order > 0) | (b >= half))(lambda: wait_block(b))
+        pull(b)
+        return carry
+
+    def wrapped(b, carry):
+        wait_block(b)
+        pull(b)
+        return carry
+
+    before_last = order == n_col - 2
+    lax.fori_loop(1, jnp.where(is_last, 1, order - cut(order)) + 1, lower, 0)
+    lax.fori_loop(order + 1, jnp.where(before_last, n_col, n_col - 1), upper, 0)
+    lax.fori_loop(0, jnp.where(before_last, cut(order) - 1, cut(order)), wrapped, 0)
+    lax.fori_loop(2, jnp.where(is_last, order - cut(order), 2), lower, 0)
     for i in range(1, n_act):
         pl.when(act_later[i])(lambda i=i: pl.semaphore_wait(act_ready.at[i], 1))
     gives0 = exchange(row_peer, lambda k: give0.at[k, 0:6], take0, row_back, 6)
     acts0 = exchange(act_peer, lambda k: line0.at[0:6], lines0, act_back, 6)
     cols1 = exchange(col_peer, lambda k: own1, got1, col_back)
-    final = jnp.where(order == n_col - 1, 0, n_col - 1)
+    final = jnp.where(
+        is_last, cut(n_col - 1), jnp.where(before_last, cut(n_col - 2) - 1, n_col - 1)
+    )
     wait_block(final)
     spread(got0[final], wide.at[0])
     last_block(wide.at[0], part, aim0, give0, gives0)
@@ -487,7 +527,13 @@
             pass_up(b).wait_send()
             return carry
 
-        lax.fori_loop(0, order, up_sent, 0)
+        lax.fori_loop(order - passed, order, up_sent, 0)
+
+    @pl.when(order == 0)
+    def _():
+        for t in range(2):
+            for copy in wraps(t):
+                copy.wait_send()
 
 
 def solution(mesh):
@@ -545,6 +591,8 @@
                 pltpu.SemaphoreType.REGULAR,
                 pltpu.SemaphoreType.REGULAR((SPAN,)),
                 pltpu.SemaphoreType.REGULAR((n_act,)),
+                pltpu.SemaphoreType.DMA((2, n_col)),
+                pltpu.SemaphoreType.REGULAR((2,)),
             ],
             compiler_params=pltpu.CompilerParams(collective_id=0, has_side_effects=True),
         )(

time: 94.2 us -> 94.2 us (level)
  no operation moved by 1% of the time
where the time goes in v4:
time: 94.2 us; the launch traced here: 93.8 us
  Pallas kernels  92.4 us (98%)
  local copies, waits for them, and re-layouts  1.38 us (1%)
    pallas_call x1, Pallas kernels, per_device(): pl.pallas_call(functools.partial(kernel, n_src, n_act), out_shape=jax.Sha...  92.4 us

profile of v4, /device:TPU:33, one launch (start us, length us, event | category | flops | bytes accessed | tf_op | source)
XLA Modules:
  0.0 93.8 jit_solution(2217501423439360221)
XLA Ops:
  0.0 92.4 %shard_map.46 = f32[12,512]{1,0:T(8,128)} custom-call(f32[12,512]{1,0:T(8,128)} %state_in.1, f32[1,512]{1,0:T(1,128)} %bitcast.3, f32[1,512]{1,0:T(1,128)} %bitcast.4, s32[1,512]{1,0:T(1,128)} %bitcast.5), custom_call_target="tpu_custom_call" | custom-call | tf_op jit(solution)/shard_map/pallas_call | solution.py:553
  92.4 1.4 %copy.6 = f32[12,512]{1,0:T(8,128)} copy(f32[12,512]{1,0:T(8,128)} %shard_map.46) | data formatting | bytes 49152

commit v5 on v4

--- a/solution.py
+++ b/solution.py
@@ -75,7 +75,7 @@
         totals = tuple(jnp.zeros((8, 128), jnp.float32) for _ in range(12))
     else:
         totals = tuple(sums[2 * pair + i, row] for i in range(2) for row in range(6))
-    totals = lax.fori_loop(0, count // 8, body, totals, unroll=2)
+    totals = lax.fori_loop(0, count // 8, body, totals, unroll=4)
     for i in range(2):
         for row in range(6):
             sums[2 * pair + i, row] = totals[6 * i + row]
@@ -552,7 +552,7 @@
 
         return pl.pallas_call(
             functools.partial(kernel, n_src, n_act),
-            out_shape=jax.ShapeDtypeStruct(star_state.shape, jnp.float32),
+            out_shape=pltpu.VMEM(star_state.shape, jnp.float32),
             in_specs=[pl.BlockSpec(memory_space=pl.ANY)] * 4,
             out_specs=vmem,
             scratch_shapes=[

time: 94.2 us -> 91.2 us (0.968)
  Pallas kernels: 92.4 us -> 90.2 us
    pallas_call x1, Pallas kernels: 92.4 us -> 90.2 us  [per_device(): pl.pallas_call(functools.partial(kernel, n_src, n_act), out_shape=pltpu.V...]
where the time goes in v5:
time: 91.2 us; the launch traced here: 90.9 us
  Pallas kernels  90.2 us (99%)
    pallas_call x1, Pallas kernels, per_device(): pl.pallas_call(functools.partial(kernel, n_src, n_act), out_shape=pltpu.V...  90.2 us

profile of v5, /device:TPU:33, one launch (start us, length us, event | category | flops | bytes accessed | tf_op | source)
XLA Modules:
  0.0 90.9 jit_solution(13522539999688571394)
XLA Ops:
  0.0 90.2 %shard_map.46 = f32[12,512]{1,0:T(8,128)S(1)} custom-call(f32[12,512]{1,0:T(8,128)} %state_in.1, f32[1,512]{1,0:T(1,128)} %bitcast.3, f32[1,512]{1,0:T(1,128)} %bitcast.4, s32[1,512]{1,0:T(1,128)} %bitcast.5), custom_call_target="tpu_custom_call" | custom-call | tf_op jit(solution)/shard_map/pallas_call | solution.py:553
  90.2 0.6 copy.6

commit v6 on v5

--- a/solution.py
+++ b/solution.py
@@ -75,7 +75,8 @@
         totals = tuple(jnp.zeros((8, 128), jnp.float32) for _ in range(12))
     else:
         totals = tuple(sums[2 * pair + i, row] for i in range(2) for row in range(6))
-    totals = lax.fori_loop(0, count // 8, body, totals, unroll=4)
+    steps = count // 8
+    totals = lax.fori_loop(0, steps, body, totals, unroll=4 if steps % 8 else 8)
     for i in range(2):
         for row in range(6):
             sums[2 * pair + i, row] = totals[6 * i + row]

time: 91.2 us -> 91 us (level)
  no operation moved by 1% of the time
where the time goes in v6:
time: 91 us; the launch traced here: 90.6 us
  Pallas kernels  90 us (99%)
    pallas_call x1, Pallas kernels, per_device(): pl.pallas_call(functools.partial(kernel, n_src, n_act), out_shape=pltpu.V...  90 us

profile of v6, /device:TPU:33, one launch (start us, length us, event | category | flops | bytes accessed | tf_op | source)
XLA Modules:
  0.0 90.6 jit_solution(11418314565961902934)
XLA Ops:
  0.0 90.0 %shard_map.46 = f32[12,512]{1,0:T(8,128)S(1)} custom-call(f32[12,512]{1,0:T(8,128)} %state_in.1, f32[1,512]{1,0:T(1,128)} %bitcast.3, f32[1,512]{1,0:T(1,128)} %bitcast.4, s32[1,512]{1,0:T(1,128)} %bitcast.5), custom_call_target="tpu_custom_call" | custom-call | tf_op jit(solution)/shard_map/pallas_call | solution.py:554
  90.0 0.6 copy.6
